TPU v7x, 32 devices: a whole 2x2x4 slice. The times are simulated.
32 devices in a mesh: gx: 8 (over y, x, core), gy: 4 (over z).
Axes of the slice: x: 2, y: 2, z: 4, core: 2. Of those that a mesh axis runs over, the one named last changes fastest.
Arguments:
- populations: float32 [19, 128, 128, 128], P(None, 'gx', 'gy'), may hold values from 0 to 10, as said below
- solid: int32 [128, 128, 128], P('gx', 'gy'), may hold values 0 or 1
Outputs:
- advanced: float32 [19, 128, 128, 128], P(None, 'gx', 'gy')
Inputs may be any that keep to these rules, and one draw needn't show every extreme that they name: populations are positive, each between 0.5 w_i 18 and 1.5 w_i 18.
All inputs are finite; a program needn't handle non-finite values. No bound on the sum of `solid` on one device may be relied on, other than what follows from the above.
Results may differ from a plain program's by a relative error of at most 0.0001.
Values sent between devices are 32-bit elements; how exact they have to be, the bound alone decides.
A program may use at most 128 MiB of HBM per device.

v0:
```python
import functools

import jax
import jax.numpy as jnp
from jax import lax
from jax.experimental import pallas as pl
from jax.experimental.pallas import tpu as pltpu
from jax.sharding import PartitionSpec as P

ITERS = 3
MESH = pl.DeviceIdType.MESH

VELOCITY = (
    (0, 0, 0),
    (1, 0, 0), (-1, 0, 0), (0, 1, 0), (0, -1, 0), (0, 0, 1), (0, 0, -1),
    (1, 1, 0), (-1, -1, 0), (1, -1, 0), (-1, 1, 0),
    (1, 0, 1), (-1, 0, -1), (1, 0, -1), (-1, 0, 1),
    (0, 1, 1), (0, -1, -1), (0, 1, -1), (0, -1, 1),
)
RELAX = 1.6
BIG = 1e37
BLOCKED = 1e34

UP_X = [1, 7, 9, 11, 13]
DOWN_X = [2, 8, 10, 12, 14]
ORDER = UP_X + DOWN_X + [0, 3, 4, 5, 6, 15, 16, 17, 18]
SLOT = {index: slot for slot, index in enumerate(ORDER)}
UP_Y = [3, 7, 10, 15, 17]
DOWN_Y = [4, 8, 9, 16, 18]
CORNERS = (7, 8, 9, 10)


def opposite(index):
    if index == 0:
        return 0
    return index + 1 if index % 2 == 1 else index - 1


def collide(f, fluid):
    total = {}
    delta = {}
    for i in range(1, 19, 2):
        total[i] = f[i] + f[i + 1]
        delta[i] = f[i] - f[i + 1]
    rho = f[0] + ((total[1] + total[3]) + (total[5] + total[7])) + (
        ((total[9] + total[11]) + (total[13] + total[15])) + total[17]
    )
    mx = (delta[1] + delta[7]) + (delta[9] + delta[11]) + delta[13]
    my = (delta[3] + delta[7]) + (delta[15] - delta[9]) + delta[17]
    mz = (delta[5] + delta[11]) + (delta[15] - delta[13]) - delta[17]
    zero = jnp.zeros_like(rho)
    scale = RELAX * 3.0 / 36.0
    mx = jnp.where(fluid, mx * scale, zero)
    my = jnp.where(fluid, my * scale, zero)
    mz = jnp.where(fluid, mz * scale, zero)
    inv = 1.0 / rho
    curve = inv * (RELAX * 4.5 / 36.0 / (scale * scale))
    base = rho * (RELAX / 36.0) - (mx * mx + my * my + mz * mz) * (
        inv * (RELAX * 1.5 / 36.0 / (scale * scale))
    )
    base = jnp.where(fluid, base, jnp.full_like(rho, BIG * RELAX / 36.0))
    post = [None] * 19
    keep = 1.0 - RELAX
    half = keep * 0.5
    post[0] = base * 12.0 + f[0] * keep
    base2 = base + base
    curve2 = curve + curve
    for i in range(1, 19, 2):
        cx, cy, cz = VELOCITY[i]
        along = None
        for c, m in ((cx, mx), (cy, my), (cz, mz)):
            if c == 0:
                continue
            if along is None:
                along = m
            else:
                along = along + m if c > 0 else along - m
        if i < 7:
            even = base2 + along * along * curve2
            odd = along + along
        else:
            even = base + along * along * curve
            odd = along
        even = even + total[i] * half
        odd = odd + delta[i] * half
        post[i] = even + odd
        post[i + 1] = even - odd
    return post


def kernel(sizes, axes, f_hbm, solid, out, field, p0, p1, p2, y_send, y_recv, in_sem, send_sem, recv_sem):
    rows, cols, gx_size, gy_size = sizes
    gx, gy = axes
    tiles = cols // 8
    buffers = (p0, p1, p2)
    me_x, me_y = lax.axis_index(gx), lax.axis_index(gy)
    up_x, down_x = lax.rem(me_x + 1, gx_size), lax.rem(me_x + gx_size - 1, gx_size)
    up_y, down_y = lax.rem(me_y + 1, gy_size), lax.rem(me_y + gy_size - 1, gy_size)
    place_x = {1: up_x, 0: me_x, -1: down_x}
    place_y = {1: up_y, 0: me_y, -1: down_y}

    def device(dx, dy):
        return {gx: place_x[dx], gy: place_y[dy]}

    inner = rows - 2
    pairs = inner // 2

    def load(start, count, sem):
        return pltpu.make_async_copy(
            f_hbm.at[:, pl.ds(start, count)], field.at[:, pl.ds(start, count)], in_sem.at[sem]
        )

    load(0, 1, 0).start()
    load(rows - 1, 1, 1).start()
    for c in range(pairs):
        load(1 + 2 * c, 2, 2 + c).start()

    barrier = pltpu.get_barrier_semaphore()
    around = [(dx, dy) for dx in (-1, 0, 1) for dy in (-1, 0, 1) if (dx, dy) != (0, 0)]
    for dx, dy in around:
        pl.semaphore_signal(barrier, inc=1, device_id=device(dx, dy), device_id_type=MESH)

    def remote(src, dst, phase, which, dx, dy):
        return pltpu.make_async_remote_copy(
            src_ref=src,
            dst_ref=dst,
            send_sem=send_sem.at[phase, which],
            recv_sem=recv_sem.at[phase, which],
            device_id=device(dx, dy),
            device_id_type=MESH,
        )

    def x_copies(phase):
        buf = buffers[phase]
        own = pl.ds(8, cols)
        copies = [
            remote(buf.at[pl.ds(0, 5), rows, own], buf.at[pl.ds(0, 5), 0, own], phase, 0, 1, 0),
            remote(buf.at[pl.ds(5, 5), 1, own], buf.at[pl.ds(5, 5), rows + 1, own], phase, 1, -1, 0),
        ]
        for k, index in enumerate(CORNERS):
            cx, cy, _ = VELOCITY[index]
            slot = SLOT[index]
            src_x, dst_x = (rows, 0) if cx > 0 else (1, rows + 1)
            src_y, dst_y = (cols, 0) if cy > 0 else (8, cols + 8)
            copies.append(
                remote(
                    buf.at[slot, src_x, pl.ds(src_y, 8)],
                    buf.at[slot, dst_x, pl.ds(dst_y, 8)],
                    phase, 4 + k, cx, cy,
                )
            )
        return copies

    def y_copies(phase):
        return [
            remote(y_send.at[phase, 0], y_recv.at[phase, 0], phase, 2, 0, 1),
            remote(y_send.at[phase, 1], y_recv.at[phase, 1], phase, 3, 0, -1),
        ]

    def pull(buf, x, t):
        top = 8 + 8 * t
        own = [buf[SLOT[i], x + 1, pl.ds(top, 8), :] for i in range(19)]
        f = [own[0]]
        for i in range(1, 19):
            cx, cy, cz = VELOCITY[i]
            if cx == 0 and cy == 0:
                value = own[i]
            else:
                value = buf[SLOT[i], x + 1 - cx, pl.ds(top - cy, 8), :]
            if cz:
                value = pltpu.roll(value, 1 if cz > 0 else value.shape[1] - 1, axis=1)
            f.append(jnp.where(value > BLOCKED, own[opposite(i)], value))
        return f

    def advance(phase, x, t):
        fluid = solid[x, pl.ds(8 * t, 8), :] == 0
        if phase == 0:
            f = [field[i, x, pl.ds(8 * t, 8), :] for i in range(19)]
        else:
            f = pull(buffers[phase - 1], x, t)
        post = collide(f, fluid)
        buf = buffers[phase]
        for i in range(19):
            buf[SLOT[i], x + 1, pl.ds(8 + 8 * t, 8), :] = post[i]
        if t == tiles - 1:
            for j, index in enumerate(UP_Y):
                y_send[phase, 0, j, pl.ds(x, 1), :] = post[index][7:8]
        if t == 0:
            for j, index in enumerate(DOWN_Y):
                y_send[phase, 1, j, pl.ds(x, 1), :] = post[index][0:1]

    def finish(x, t):
        fluid = solid[x, pl.ds(8 * t, 8), :] == 0
        f = pull(buffers[ITERS - 1], x, t)
        for i in range(19):
            kept = field[i, x, pl.ds(8 * t, 8), :]
            out[i, x, pl.ds(8 * t, 8), :] = jnp.where(fluid, f[i], kept)

    edge_tiles = sorted({0, tiles - 1})
    inner_tiles = [t for t in range(tiles) if t not in edge_tiles]

    def loop(body, which):
        if not which:
            return

        def step(c, carry):
            for dx in range(2):
                for t in which:
                    body(1 + 2 * c + dx, t)
            return carry

        lax.fori_loop(0, pairs, step, 0)

    def merge(phase):
        buf = buffers[phase]

        def step(x, carry):
            for j, index in enumerate(UP_Y):
                buf[SLOT[index], x + 1, pl.ds(7, 1), :] = y_recv[phase, 0, j, pl.ds(x, 1), :]
            for j, index in enumerate(DOWN_Y):
                buf[SLOT[index], x + 1, pl.ds(cols + 8, 1), :] = y_recv[phase, 1, j, pl.ds(x, 1), :]
            return carry

        lax.fori_loop(0, rows, step, 0)

    for phase in range(ITERS):
        if phase == 0:
            load(0, 1, 0).wait()
            load(rows - 1, 1, 1).wait()
        else:
            for copy in y_copies(phase - 1):
                copy.wait_recv()
            merge(phase - 1)
            for copy in x_copies(phase - 1):
                copy.wait_recv()
        for x in (0, rows - 1):
            for t in range(tiles):
                advance(phase, x, t)
        if phase == 0:
            pl.semaphore_wait(barrier, len(around))
        for copy in x_copies(phase):
            copy.start()
        if phase == 0:
            for c in range(pairs):
                load(1 + 2 * c, 2, 2 + c).wait()
        loop(functools.partial(advance, phase), edge_tiles)
        for copy in y_copies(phase):
            copy.start()
        loop(functools.partial(advance, phase), inner_tiles)

    loop(finish, inner_tiles)
    last = ITERS - 1
    for copy in y_copies(last):
        copy.wait_recv()
    merge(last)
    loop(finish, edge_tiles)
    for copy in x_copies(last):
        copy.wait_recv()
    for x in (0, rows - 1):
        for t in range(tiles):
            finish(x, t)
    for phase in range(ITERS):
        for copy in x_copies(phase) + y_copies(phase):
            copy.wait_send()


def solution(mesh):
    gx, gy = mesh.axis_names
    gx_size, gy_size = mesh.shape[gx], mesh.shape[gy]

    def local(populations, solid):
        count, rows, cols, lanes = populations.shape
        f32 = jnp.float32
        padded = pltpu.VMEM((count, rows + 2, cols + 16, lanes), f32)
        return pl.pallas_call(
            functools.partial(kernel, (rows, cols, gx_size, gy_size), (gx, gy)),
            out_shape=jax.ShapeDtypeStruct(populations.shape, f32),
            in_specs=[pl.BlockSpec(memory_space=pltpu.HBM), pl.BlockSpec(memory_space=pltpu.VMEM)],
            out_specs=pl.BlockSpec(memory_space=pltpu.VMEM),
            scratch_shapes=[
                pltpu.VMEM((count, rows, cols, lanes), f32),
                padded,
                padded,
                padded,
                pltpu.VMEM((ITERS, 2, 5, rows, lanes), f32),
                pltpu.VMEM((ITERS, 2, 5, rows, lanes), f32),
                pltpu.SemaphoreType.DMA((2 + (rows - 2) // 2,)),
                pltpu.SemaphoreType.DMA((ITERS, 8)),
                pltpu.SemaphoreType.DMA((ITERS, 8)),
            ],
            compiler_params=pltpu.CompilerParams(
                collective_id=0, has_side_effects=True, vmem_limit_bytes=44 * 1024 * 1024
            ),
        )(populations, solid)

    return jax.shard_map(
        local,
        mesh=mesh,
        in_specs=(P(None, gx, gy, None), P(gx, gy, None)),
        out_specs=P(None, gx, gy, None),
        check_vma=False,
    )
```

profile of v0, /device:TPU:0, one launch (start us, length us, event | category | flops | bytes accessed | tf_op | source)
XLA Modules:
  0.0 29.1 jit_solution(10611515754279171667)
XLA Ops:
  0.0 0.0 copy-start
  0.0 2.4 %copy-done = f32[19,16,32,128]{3,2,1,0:T(8,128)S(1)} copy-done((f32[19,16,32,128]{3,2,1,0:T(8,128)S(1)}, f32[19,16,32,128]{3,2,1,0:T(8,128)}, u32[]{:S(2)}) %copy-start) | copy-done | bytes 4980760
  2.4 0.0 copy-start.1
  2.4 0.9 %copy-done.1 = s32[16,32,128]{2,1,0:T(8,128)S(1)} copy-done((s32[16,32,128]{2,1,0:T(8,128)S(1)}, s32[16,32,128]{2,1,0:T(8,128)}, u32[]{:S(2)}) %copy-start.1) | copy-done | bytes 262168
  3.4 23.5 %shard_map.28 = f32[19,16,32,128]{3,2,1,0:T(8,128)S(1)} custom-call(f32[19,16,32,128]{3,2,1,0:T(8,128)S(1)} %copy-done, s32[16,32,128]{2,1,0:T(8,128)S(1)} %copy-done.1), custom_call_target="tpu_custom_call" | custom-call | tf_op jit(solution)/shard_map/pallas_call | solution.py:275
  26.8 2.3 %copy.4 = f32[19,16,32,128]{3,2,1,0:T(8,128)} copy(f32[19,16,32,128]{3,2,1,0:T(8,128)S(1)} %shard_map.28) | data formatting | bytes 9961472
Async XLA Ops:
  0.0 2.4 %copy-start = (f32[19,16,32,128]{3,2,1,0:T(8,128)S(1)}, f32[19,16,32,128]{3,2,1,0:T(8,128)}, u32[]{:S(2)}) copy-start(f32[19,16,32,128]{3,2,1,0:T(8,128)} %f_hbm.1) | copy-start | bytes 14942212
  2.4 0.9 %copy-start.1 = (s32[16,32,128]{2,1,0:T(8,128)S(1)}, s32[16,32,128]{2,1,0:T(8,128)}, u32[]{:S(2)}) copy-start(s32[16,32,128]{2,1,0:T(8,128)} %solid.1) | copy-start | bytes 786436
where the time goes:
time: 29.3 us; the launch traced here: 29.1 us
  Pallas kernels  23.5 us (80%)
  local copies, waits for them, and re-layouts  5.63 us (19%)
    pallas_call x1, Pallas kernels, local(): pl.pallas_call(functools.partial(kernel, (rows, cols, gx_size, gy_size),...  23.5 us
    unnamed x5, local copies, waits for them, and re-layouts  5.63 us

commit v1 on v0

--- a/solution.py
+++ b/solution.py
@@ -88,7 +88,7 @@
     return post
 
 
-def kernel(sizes, axes, f_hbm, solid, out, field, p0, p1, p2, y_send, y_recv, in_sem, send_sem, recv_sem):
+def kernel(sizes, axes, f_hbm, solid_hbm, out, field, solid, p0, p1, p2, y_send, y_recv, in_sem, send_sem, recv_sem):
     rows, cols, gx_size, gy_size = sizes
     gx, gy = axes
     tiles = cols // 8
@@ -104,21 +104,24 @@
 
     inner = rows - 2
     pairs = inner // 2
+    half = rows // 2
 
     def load(start, count, sem):
         return pltpu.make_async_copy(
             f_hbm.at[:, pl.ds(start, count)], field.at[:, pl.ds(start, count)], in_sem.at[sem]
         )
 
+    barrier = pltpu.get_barrier_semaphore()
+    around = [(dx, dy) for dx in (-1, 0, 1) for dy in (-1, 0, 1) if (dx, dy) != (0, 0)]
+    for dx, dy in around:
+        pl.semaphore_signal(barrier, inc=1, device_id=device(dx, dy), device_id_type=MESH)
+
+    load_solid = pltpu.make_async_copy(solid_hbm, solid, in_sem.at[2 + pairs])
+    load_solid.start()
     load(0, 1, 0).start()
     load(rows - 1, 1, 1).start()
     for c in range(pairs):
         load(1 + 2 * c, 2, 2 + c).start()
-
-    barrier = pltpu.get_barrier_semaphore()
-    around = [(dx, dy) for dx in (-1, 0, 1) for dy in (-1, 0, 1) if (dx, dy) != (0, 0)]
-    for dx, dy in around:
-        pl.semaphore_signal(barrier, inc=1, device_id=device(dx, dy), device_id_type=MESH)
 
     def remote(src, dst, phase, which, dx, dy):
         return pltpu.make_async_remote_copy(
@@ -130,31 +133,38 @@
             device_id_type=MESH,
         )
 
-    def x_copies(phase):
+    def x_copies(phase, side):
         buf = buffers[phase]
         own = pl.ds(8, cols)
+        src_x, dst_x, slots = (rows, 0, pl.ds(0, 5)) if side > 0 else (1, rows + 1, pl.ds(5, 5))
         copies = [
-            remote(buf.at[pl.ds(0, 5), rows, own], buf.at[pl.ds(0, 5), 0, own], phase, 0, 1, 0),
-            remote(buf.at[pl.ds(5, 5), 1, own], buf.at[pl.ds(5, 5), rows + 1, own], phase, 1, -1, 0),
+            remote(
+                buf.at[slots, src_x, own], buf.at[slots, dst_x, own], phase, 0 if side > 0 else 1, side, 0
+            )
         ]
         for k, index in enumerate(CORNERS):
             cx, cy, _ = VELOCITY[index]
+            if cx != side:
+                continue
             slot = SLOT[index]
-            src_x, dst_x = (rows, 0) if cx > 0 else (1, rows + 1)
             src_y, dst_y = (cols, 0) if cy > 0 else (8, cols + 8)
             copies.append(
                 remote(
                     buf.at[slot, src_x, pl.ds(src_y, 8)],
                     buf.at[slot, dst_x, pl.ds(dst_y, 8)],
-                    phase, 4 + k, cx, cy,
+                    phase, 2 + k, cx, cy,
                 )
             )
         return copies
 
-    def y_copies(phase):
+    def y_copies(phase, chunk):
+        planes = pl.ds(chunk * half, half)
         return [
-            remote(y_send.at[phase, 0], y_recv.at[phase, 0], phase, 2, 0, 1),
-            remote(y_send.at[phase, 1], y_recv.at[phase, 1], phase, 3, 0, -1),
+            remote(
+                y_send.at[phase, side, :, planes], y_recv.at[phase, side, :, planes],
+                phase, 6 + 2 * side + chunk, 0, 1 - 2 * side,
+            )
+            for side in range(2)
         ]
 
     def pull(buf, x, t):
@@ -199,68 +209,90 @@
     edge_tiles = sorted({0, tiles - 1})
     inner_tiles = [t for t in range(tiles) if t not in edge_tiles]
 
-    def loop(body, which):
+    def loop(body, which, first=1, stop=rows - 1):
         if not which:
             return
 
         def step(c, carry):
             for dx in range(2):
                 for t in which:
-                    body(1 + 2 * c + dx, t)
+                    body(first + 2 * c + dx, t)
             return carry
 
-        lax.fori_loop(0, pairs, step, 0)
-
-    def merge(phase):
+        lax.fori_loop(0, (stop - first) // 2, step, 0)
+
+    def merge(phase, chunk):
         buf = buffers[phase]
 
-        def step(x, carry):
-            for j, index in enumerate(UP_Y):
-                buf[SLOT[index], x + 1, pl.ds(7, 1), :] = y_recv[phase, 0, j, pl.ds(x, 1), :]
-            for j, index in enumerate(DOWN_Y):
-                buf[SLOT[index], x + 1, pl.ds(cols + 8, 1), :] = y_recv[phase, 1, j, pl.ds(x, 1), :]
+        def step(c, carry):
+            for dx in range(2):
+                x = chunk * half + 2 * c + dx
+                for j, index in enumerate(UP_Y):
+                    buf[SLOT[index], x + 1, pl.ds(7, 1), :] = y_recv[phase, 0, j, pl.ds(x, 1), :]
+                for j, index in enumerate(DOWN_Y):
+                    buf[SLOT[index], x + 1, pl.ds(cols + 8, 1), :] = y_recv[phase, 1, j, pl.ds(x, 1), :]
             return carry
 
-        lax.fori_loop(0, rows, step, 0)
+        lax.fori_loop(0, half // 2, step, 0)
+
+    def plane(body, x):
+        for t in range(tiles):
+            body(x, t)
+
+    def arrive(copies):
+        for copy in copies:
+            copy.wait_recv()
+
+    def send(copies):
+        for copy in copies:
+            copy.start()
 
     for phase in range(ITERS):
+        body = functools.partial(advance, phase)
         if phase == 0:
+            load_solid.wait()
             load(0, 1, 0).wait()
+            plane(body, 0)
+            pl.semaphore_wait(barrier, len(around))
+            send(x_copies(phase, -1))
             load(rows - 1, 1, 1).wait()
-        else:
-            for copy in y_copies(phase - 1):
-                copy.wait_recv()
-            merge(phase - 1)
-            for copy in x_copies(phase - 1):
-                copy.wait_recv()
-        for x in (0, rows - 1):
-            for t in range(tiles):
-                advance(phase, x, t)
-        if phase == 0:
-            pl.semaphore_wait(barrier, len(around))
-        for copy in x_copies(phase):
-            copy.start()
-        if phase == 0:
+            plane(body, rows - 1)
+            send(x_copies(phase, 1))
             for c in range(pairs):
                 load(1 + 2 * c, 2, 2 + c).wait()
-        loop(functools.partial(advance, phase), edge_tiles)
-        for copy in y_copies(phase):
-            copy.start()
-        loop(functools.partial(advance, phase), inner_tiles)
-
+            loop(body, edge_tiles, 1, half - 1)
+        else:
+            arrive(y_copies(phase - 1, 0))
+            merge(phase - 1, 0)
+            arrive(x_copies(phase - 1, 1))
+            plane(body, 0)
+            send(x_copies(phase, -1))
+            loop(body, edge_tiles, 1, half - 1)
+            arrive(y_copies(phase - 1, 1))
+            merge(phase - 1, 1)
+            arrive(x_copies(phase - 1, -1))
+            plane(body, rows - 1)
+            send(x_copies(phase, 1))
+        loop(body, edge_tiles, half - 1, half + 1)
+        send(y_copies(phase, 0))
+        loop(body, edge_tiles, half + 1, rows - 1)
+        send(y_copies(phase, 1))
+        loop(body, inner_tiles)
+
+    last = ITERS - 1
     loop(finish, inner_tiles)
-    last = ITERS - 1
-    for copy in y_copies(last):
-        copy.wait_recv()
-    merge(last)
-    loop(finish, edge_tiles)
-    for copy in x_copies(last):
-        copy.wait_recv()
-    for x in (0, rows - 1):
-        for t in range(tiles):
-            finish(x, t)
+    arrive(y_copies(last, 0))
+    merge(last, 0)
+    arrive(x_copies(last, 1))
+    plane(finish, 0)
+    loop(finish, edge_tiles, 1, half - 1)
+    arrive(y_copies(last, 1))
+    merge(last, 1)
+    loop(finish, edge_tiles, half - 1, rows - 1)
+    arrive(x_copies(last, -1))
+    plane(finish, rows - 1)
     for phase in range(ITERS):
-        for copy in x_copies(phase) + y_copies(phase):
+        for copy in x_copies(phase, 1) + x_copies(phase, -1) + y_copies(phase, 0) + y_copies(phase, 1):
             copy.wait_send()
 
 
@@ -275,23 +307,27 @@
         return pl.pallas_call(
             functools.partial(kernel, (rows, cols, gx_size, gy_size), (gx, gy)),
             out_shape=jax.ShapeDtypeStruct(populations.shape, f32),
-            in_specs=[pl.BlockSpec(memory_space=pltpu.HBM), pl.BlockSpec(memory_space=pltpu.VMEM)],
+            in_specs=[pl.BlockSpec(memory_space=pltpu.HBM)] * 2,
             out_specs=pl.BlockSpec(memory_space=pltpu.VMEM),
             scratch_shapes=[
                 pltpu.VMEM((count, rows, cols, lanes), f32),
+                pltpu.VMEM((rows, cols, lanes), jnp.int32),
                 padded,
                 padded,
                 padded,
                 pltpu.VMEM((ITERS, 2, 5, rows, lanes), f32),
                 pltpu.VMEM((ITERS, 2, 5, rows, lanes), f32),
-                pltpu.SemaphoreType.DMA((2 + (rows - 2) // 2,)),
-                pltpu.SemaphoreType.DMA((ITERS, 8)),
-                pltpu.SemaphoreType.DMA((ITERS, 8)),
+                pltpu.SemaphoreType.DMA((3 + (rows - 2) // 2,)),
+                pltpu.SemaphoreType.DMA((ITERS, 10)),
+                pltpu.SemaphoreType.DMA((ITERS, 10)),
             ],
             compiler_params=pltpu.CompilerParams(
-                collective_id=0, has_side_effects=True, vmem_limit_bytes=44 * 1024 * 1024
+                collective_id=0, has_side_effects=True, vmem_limit_bytes=46 * 1024 * 1024
             ),
-        )(populations, solid)
+        )(
+            pltpu.with_memory_space_constraint(populations, pltpu.HBM),
+            pltpu.with_memory_space_constraint(solid, pltpu.HBM),
+        )
 
     return jax.shard_map(
         local,

time: 29.3 us -> 24.2 us (0.83)
  local copies, waits for them, and re-layouts: 5.63 us -> 2.27 us
  Pallas kernels: 23.5 us -> 21.7 us
    unnamed x5 -> x1, local copies, waits for them, and re-layouts: 5.63 us -> 2.27 us
    pallas_call x1, Pallas kernels: 23.5 us -> 21.7 us  [local(): pl.pallas_call(functools.partial(kernel, (rows, cols, gx_size, gy_size),...]
where the time goes in v1:
time: 24.2 us; the launch traced here: 24 us
  Pallas kernels  21.7 us (90%)
  local copies, waits for them, and re-layouts  2.27 us (9%)
    pallas_call x1, Pallas kernels, local(): pl.pallas_call(functools.partial(kernel, (rows, cols, gx_size, gy_size),...  21.7 us
    unnamed x1, local copies, waits for them, and re-layouts  2.27 us

profile of v1, /device:TPU:0, one launch (start us, length us, event | category | flops | bytes accessed | tf_op | source)
XLA Modules:
  0.0 24.0 jit_solution(9386625766305786391)
XLA Ops:
  0.0 21.7 %shard_map.28 = f32[19,16,32,128]{3,2,1,0:T(8,128)S(1)} custom-call(f32[19,16,32,128]{3,2,1,0:T(8,128)} %f_hbm.1, s32[16,32,128]{2,1,0:T(8,128)} %solid_hbm.1), custom_call_target="tpu_custom_call" | custom-call | tf_op jit(solution)/shard_map/pallas_call | solution.py:307
  21.7 2.3 %copy.4 = f32[19,16,32,128]{3,2,1,0:T(8,128)} copy(f32[19,16,32,128]{3,2,1,0:T(8,128)S(1)} %shard_map.28) | data formatting | bytes 9961472

commit v2 on v1

--- a/solution.py
+++ b/solution.py
@@ -247,6 +247,12 @@
         for copy in copies:
             copy.start()
 
+    first_pairs = (half - 2) // 2
+
+    def loaded(low, high):
+        for c in range(low, high):
+            load(1 + 2 * c, 2, 2 + c).wait()
+
     for phase in range(ITERS):
         body = functools.partial(advance, phase)
         if phase == 0:
@@ -258,9 +264,9 @@
             load(rows - 1, 1, 1).wait()
             plane(body, rows - 1)
             send(x_copies(phase, 1))
-            for c in range(pairs):
-                load(1 + 2 * c, 2, 2 + c).wait()
+            loaded(0, first_pairs)
             loop(body, edge_tiles, 1, half - 1)
+            loaded(first_pairs, first_pairs + 1)
         else:
             arrive(y_copies(phase - 1, 0))
             merge(phase - 1, 0)
@@ -275,6 +281,8 @@
             send(x_copies(phase, 1))
         loop(body, edge_tiles, half - 1, half + 1)
         send(y_copies(phase, 0))
+        if phase == 0:
+            loaded(first_pairs + 1, pairs)
         loop(body, edge_tiles, half + 1, rows - 1)
         send(y_copies(phase, 1))
         loop(body, inner_tiles)

time: 24.2 us -> 24.2 us (level)
  no operation moved by 1% of the time
where the time goes in v2:
time: 24.2 us; the launch traced here: 24 us
  Pallas kernels  21.7 us (90%)
  local copies, waits for them, and re-layouts  2.27 us (9%)
    pallas_call x1, Pallas kernels, local(): pl.pallas_call(functools.partial(kernel, (rows, cols, gx_size, gy_size),...  21.7 us
    unnamed x1, local copies, waits for them, and re-layouts  2.27 us

profile of v2, /device:TPU:0, one launch (start us, length us, event | category | flops | bytes accessed | tf_op | source)
XLA Modules:
  0.0 24.0 jit_solution(2183658976167638483)
XLA Ops:
  0.0 21.7 %shard_map.28 = f32[19,16,32,128]{3,2,1,0:T(8,128)S(1)} custom-call(f32[19,16,32,128]{3,2,1,0:T(8,128)} %f_hbm.1, s32[16,32,128]{2,1,0:T(8,128)} %solid_hbm.1), custom_call_target="tpu_custom_call" | custom-call | tf_op jit(solution)/shard_map/pallas_call | solution.py:315
  21.7 2.3 %copy.4 = f32[19,16,32,128]{3,2,1,0:T(8,128)} copy(f32[19,16,32,128]{3,2,1,0:T(8,128)S(1)} %shard_map.28) | data formatting | bytes 9961472
